TPU v7x, 32 devices: a whole 2x2x4 slice. The times are simulated.
32 devices in a mesh: grp: 4 (over z), row: 4 (over x, core), col: 2 (over y).
Axes of the slice: x: 2, y: 2, z: 4, core: 2. Of those that a mesh axis runs over, the one named last changes fastest.
Arguments:
- acts: bfloat16 [768, 8192], P('grp', 'col'), may hold values from -6 to 6
- grads: bfloat16 [768, 28672], P('grp', ('row', 'col')), may hold values from -6 to 6
- basis_in: bfloat16 [8192, 4096], P('col', 'row'), may hold values from -0.0625 to 0.0625
- basis_out: bfloat16 [4, 7168, 14336], P('row', 'grp', 'col'), may hold values from -0.03125 to 0.03125
- lengths: int32 [4, 2], P('grp'), may hold values from 1 to 96, 144 in all within a row
Outputs:
- eigenvalues: float32 [14336, 4096], P('col', 'row')
Inputs may be any that keep to these rules, and one draw needn't show every extreme that they name: The 2 lengths of each index of grp sum to exactly 144, and none exceeds 96.
All inputs are finite; a program needn't handle non-finite values.
Results may differ from a plain program's by a relative error of at most 0.006.
Values may be sent and summed in bfloat16 or wider, within the bound.
A program may use at most 256 MiB of HBM per device.

v0:
```python
import jax
import jax.numpy as jnp
from jax import lax
from jax.sharding import PartitionSpec as P

LEN = 96
VALID = 144


def outer_square(left, right):
    block = lax.dot_general(
        left, right, (((0,), (0,)), ((), ())), preferred_element_type=jnp.float32
    )
    return block * block


def per_device(acts, grads, basis_in, basis_out, lengths):
    seq_lens = lengths[0]
    count = seq_lens.shape[0]
    partial_in = jnp.dot(acts, basis_in, preferred_element_type=jnp.float32)
    proj_in = lax.psum(partial_in, "col").astype(jnp.bfloat16)
    ends = jnp.cumsum(seq_lens)
    starts = ends - seq_lens
    slot_ids = jnp.arange(VALID, dtype=jnp.int32)
    segment = jnp.sum((slot_ids[:, None] >= ends[None, :]).astype(jnp.int32), axis=1)
    member = segment[:, None] == jnp.arange(count, dtype=jnp.int32)[None, :]
    offset = jnp.sum(jnp.where(member, starts[None, :], 0), axis=1)
    source = segment * LEN + slot_ids - offset
    packed = jnp.take(grads, source, axis=0)
    gathered = lax.all_gather(packed, "col", axis=1, tiled=True)
    proj_in = jnp.take(proj_in, source, axis=0)
    partial_out = jnp.dot(
        gathered,
        lax.all_gather(basis_out, "grp", axis=1, tiled=True)[0],
        preferred_element_type=jnp.float32,
    )
    proj_out = lax.psum(partial_out, "row").astype(jnp.bfloat16)
    slot_pos = jnp.arange(LEN, dtype=jnp.int32)
    total = jnp.zeros((proj_out.shape[1], proj_in.shape[1]), jnp.float32)
    padded_out = jnp.concatenate(
        [proj_out, jnp.zeros((LEN, proj_out.shape[1]), jnp.bfloat16)], axis=0
    )
    padded_in = jnp.concatenate([proj_in, jnp.zeros((LEN, proj_in.shape[1]), jnp.bfloat16)], axis=0)
    for seq in range(count):
        keep = (slot_pos < seq_lens[seq]).astype(jnp.bfloat16)
        piece_out = lax.dynamic_slice_in_dim(padded_out, starts[seq], LEN, 0)
        piece_in = lax.dynamic_slice_in_dim(padded_in, starts[seq], LEN, 0)
        total = total + outer_square(piece_out * keep[:, None], piece_in)
    summed = lax.psum(total, "grp")
    return summed / (lax.axis_size("grp") * count * LEN)


def solution(mesh):
    in_specs = (
        P("grp", "col"),
        P("grp", ("row", "col")),
        P("col", "row"),
        P("row", "grp", "col"),
        P("grp", None),
    )
    out_specs = P("col", "row")
    return jax.shard_map(
        per_device, mesh=mesh, in_specs=in_specs, out_specs=out_specs, check_vma=False
    )
```

profile of v0, /device:TPU:0, one launch (start us, length us, event | category | flops | bytes accessed | tf_op | source)
XLA Modules:
  0.0 2906.0 jit_solution(11868883489751046661)
XLA Ops:
  6.5 0.0 copy-start
  6.5 0.0 all-gather.3.cloned.1.call-start
  6.5 0.9 reduce-window.4
  7.5 0.7 fusion.13
  8.1 0.1 fusion.9
  8.2 0.1 fusion.10
  8.4 3.7 gather_fusion
  12.1 1.1 broadcast_select_fusion
  13.2 0.0 all-gather.3.cloned.1.call-update
  13.3 0.0 copy-start.2
  13.3 0.0 all-gather.5.cloned.1.call-start
  13.3 0.7 all-gather.5.cloned.1.call-update
  14.0 0.0 all-reduce.6.cloned.1.call-start
  14.1 0.0 copy-done.2
  14.1 0.6 fusion.17
  17.1 0.0 copy-done
  17.1 5.2 fusion.18
  22.2 43.5 %all-reduce.8 = bf16[192,1024]{1,0:T(8,128)(2,1)S(1)} all-reduce(f32[192,1024]{1,0:T(8,128)S(1)} %fusion.18), channel_id=1, replica_groups=mesh['grp'=4,'row'=4,'col'=2] {'col'}, use_global_device_ids=true, to_apply=%region_4.5 | all-reduce | flops 196608 | bytes 1179648 | tf_op jit(solution)/shard_map/psum | solution.py:21
  65.7 0.9 gather_fusion.1
  67.8 0.6 fusion.16
  68.4 0.6 compare_convert_fusion.2
  69.0 0.6 compare_convert_fusion.1
  69.6 0.1 broadcast_select_fusion.1
  69.7 0.0 all-gather.3.cloned.1.call-done
  69.7 1693.3 %all-gather.5.cloned.1.call-done = bf16[1,7168,7168]{2,1,0:T(8,128)(2,1)} async-done(((bf16[1,1792,7168]{2,1,0:T(8,128)(2,1)}), bf16[1,7168,7168]{2,1,0:T(8,128)(2,1)}) %all-gather.5.cloned.1.call-update) | async-done | bytes 102760464 | tf_op jit(solution)/shard_map/all_gather | solution.py:34
  1763.0 37.1 %fusion = f32[144,7168]{1,0:T(8,128)} fusion(bf16[144,7168]{1,0:T(8,128)(2,1)} %all-gather.3.cloned.1.call-done, bf16[1,7168,7168]{2,1,0:T(8,128)(2,1)} %all-gather.5.cloned.1.call-done), kind=kOutput, calls=%fused_computation.2 | convolution fusion | flops 14797504512 | bytes 108953600 | tf_op jit(solution)/shard_map/dot_general | solution.py:32
  1800.1 76.2 %all-reduce.7 = bf16[144,7168]{1,0:T(8,128)(2,1)} all-reduce(f32[144,7168]{1,0:T(8,128)} %fusion), channel_id=1, replica_groups=mesh['grp'=4,'row'=4,'col'=2] {'row'}, use_global_device_ids=true, to_apply=%region_3.4 | all-reduce | flops 1032192 | bytes 6193152 | tf_op jit(solution)/shard_map/psum | solution.py:37
  1876.3 13.9 fusion.3
  1890.2 19.6 multiply_add_fusion
  1909.8 0.0 all-reduce.6.cloned.1.call-update
  1909.8 966.3 %all-reduce.6.cloned.1.call-done = f32[7168,1024]{1,0:T(8,128)} async-done(((f32[7168,1024]{1,0:T(8,128)}), f32[7168,1024]{1,0:T(8,128)}) %all-reduce.6.cloned.1.call-update) | async-done | bytes 29360144 | tf_op jit(solution)/shard_map/psum | solution.py:49
  2876.1 0.0 copy-start.1
  2876.1 23.3 broadcast_multiply_fusion
  2899.4 0.0 copy-done.1
  (5 shorter events, 0.0 us)
Async XLA Ops:
  6.5 10.5 copy-start
  6.5 63.2 %all-gather.3.cloned.1.call-start = ((), (), s32[]{:S(2)}) async-start(), calls=%async_computation | async-start | bytes 3096576 | tf_op jit(solution)/shard_map/all_gather | solution.py:30
  13.3 0.8 copy-start.2
  13.3 1749.7 %all-gather.5.cloned.1.call-start = ((), (), s32[]{:S(2)}) async-start(), calls=%async_computation.1 | async-start | bytes 128450560 | tf_op jit(solution)/shard_map/all_gather | solution.py:34
  14.0 2862.1 %all-reduce.6.cloned.1.call-start = ((), (), s32[]{:S(2)}) async-start(), calls=%async_computation.2 | async-start | bytes 58720256 | tf_op jit(solution)/shard_map/psum | solution.py:49
  2876.1 23.3 copy-start.1
Sparse Core Ops, SparseCore 0:
  13.4 52.2 all-gather.2
  67.3 1695.6 all-gather.4
  1909.9 966.1 all-reduce.5
where the time goes:
time: 2910 us
  waiting for transfers between devices  2660 us (91%)
  blocking collectives  120 us (4%)
  matrix products  75.7 us (3%)
    all_gather x1, waiting for transfers between devices, per_device(): lax.all_gather(basis_out, 'grp', axis=1, tiled=True)[0]  1690 us
    psum x1, waiting for transfers between devices, per_device(): summed = lax.psum(total, 'grp')  966 us
    psum x1, blocking collectives, per_device(): proj_out = lax.psum(partial_out, 'row').astype(jnp.bfloat16)  76.2 us
  transfers between devices with their start and end apart: 3, of which 2 were waited for; matrix products, arithmetic and copies ran while one was open for 0% of the time, Pallas kernels for 0%

commit v1 on v0

--- a/solution.py
+++ b/solution.py
@@ -1,10 +1,20 @@
+import functools
 import jax
 import jax.numpy as jnp
 from jax import lax
 from jax.sharding import PartitionSpec as P
+from jax.lax import all_gather
 
 LEN = 96
 VALID = 144
+
+
+def resolve_map(raw, comm_axis):
+    out_arr = jnp.concatenate(all_gather(raw, comm_axis), axis=1)
+    return out_arr
+
+
+connect_members_all = functools.partial(resolve_map, comm_axis="grp")
 
 
 def outer_square(left, right):
@@ -30,9 +40,7 @@
     gathered = lax.all_gather(packed, "col", axis=1, tiled=True)
     proj_in = jnp.take(proj_in, source, axis=0)
     partial_out = jnp.dot(
-        gathered,
-        lax.all_gather(basis_out, "grp", axis=1, tiled=True)[0],
-        preferred_element_type=jnp.float32,
+        gathered, connect_members_all(basis_out)[0], preferred_element_type=jnp.float32
     )
     proj_out = lax.psum(partial_out, "row").astype(jnp.bfloat16)
     slot_pos = jnp.arange(LEN, dtype=jnp.int32)

time: 2910 us -> 2910 us (level)
  no operation moved by 1% of the time
where the time goes in v1:
time: 2910 us
  waiting for transfers between devices  2660 us (91%)
  blocking collectives  120 us (4%)
  matrix products  75.7 us (3%)
    all_gather x1, waiting for transfers between devices, resolve_map(): out_arr = jnp.concatenate(all_gather(raw, comm_axis), axis=1)  1690 us
    psum x1, waiting for transfers between devices, per_device(): summed = lax.psum(total, 'grp')  966 us
    psum x1, blocking collectives, per_device(): proj_out = lax.psum(partial_out, 'row').astype(jnp.bfloat16)  76.2 us
  transfers between devices with their start and end apart: 3, of which 2 were waited for; matrix products, arithmetic and copies ran while one was open for 0% of the time, Pallas kernels for 0%

profile of v1, /device:TPU:0, one launch (start us, length us, event | category | flops | bytes accessed | tf_op | source)
XLA Modules:
  0.0 2906.0 jit_solution(11868883489751046661)
XLA Ops:
  6.5 0.0 copy-start
  6.5 0.0 all-gather.4.cloned.1.call-start
  6.5 0.9 reduce-window.4
  7.5 0.7 fusion.11
  8.1 0.1 fusion.7
  8.2 0.1 fusion.8
  8.4 3.7 gather_fusion
  12.1 1.1 broadcast_select_fusion
  13.2 0.0 all-gather.4.cloned.1.call-update
  13.3 0.0 copy-start.2
  13.3 0.0 all-gather.6.cloned.1.call-start
  13.3 0.7 all-gather.6.cloned.1.call-update
  14.0 0.0 all-reduce.6.cloned.1.call-start
  14.1 0.0 copy-done.2
  14.1 0.6 fusion.15
  17.1 0.0 copy-done
  17.1 5.2 fusion.17
  22.2 43.5 %all-reduce.8 = bf16[192,1024]{1,0:T(8,128)(2,1)S(1)} all-reduce(f32[192,1024]{1,0:T(8,128)S(1)} %fusion.17), channel_id=1, replica_groups=mesh['grp'=4,'row'=4,'col'=2] {'col'}, use_global_device_ids=true, to_apply=%region_4.5 | all-reduce | flops 196608 | bytes 1179648 | tf_op jit(solution)/shard_map/psum | solution.py:31
  65.7 0.9 gather_fusion.1
  67.8 0.6 fusion.14
  68.4 0.6 compare_convert_fusion.2
  69.0 0.6 compare_convert_fusion.1
  69.6 0.1 broadcast_select_fusion.1
  69.7 0.0 all-gather.4.cloned.1.call-done
  69.7 1693.3 %all-gather.6.cloned.1.call-done = bf16[4,1792,7168]{2,1,0:T(8,128)(2,1)} async-done(((bf16[1,1792,7168]{2,1,0:T(8,128)(2,1)}), bf16[4,1792,7168]{2,1,0:T(8,128)(2,1)}) %all-gather.6.cloned.1.call-update) | async-done | bytes 102760464 | tf_op jit(solution)/shard_map/all_gather | solution.py:13
  1763.0 37.1 %fusion.16 = f32[144,7168]{1,0:T(8,128)} fusion(bf16[144,7168]{1,0:T(8,128)(2,1)} %all-gather.4.cloned.1.call-done, bf16[7168,7168]{1,0:T(8,128)(2,1)} %bitcast.7), kind=kOutput, calls=%fused_computation.35 | convolution fusion | flops 14797504512 | bytes 108953600 | tf_op jit(solution)/shard_map/dot_general | solution.py:42
  1800.1 76.2 %all-reduce.7 = bf16[144,7168]{1,0:T(8,128)(2,1)} all-reduce(f32[144,7168]{1,0:T(8,128)} %fusion.16), channel_id=1, replica_groups=mesh['grp'=4,'row'=4,'col'=2] {'row'}, use_global_device_ids=true, to_apply=%region_3.4 | all-reduce | flops 1032192 | bytes 6193152 | tf_op jit(solution)/shard_map/psum | solution.py:45
  1876.3 13.9 fusion.1
  1890.2 19.6 multiply_add_fusion
  1909.8 0.0 all-reduce.6.cloned.1.call-update
  1909.8 966.3 %all-reduce.6.cloned.1.call-done = f32[7168,1024]{1,0:T(8,128)} async-done(((f32[7168,1024]{1,0:T(8,128)}), f32[7168,1024]{1,0:T(8,128)}) %all-reduce.6.cloned.1.call-update) | async-done | bytes 29360144 | tf_op jit(solution)/shard_map/psum | solution.py:57
  2876.1 0.0 copy-start.1
  2876.1 23.3 broadcast_multiply_fusion
  2899.4 0.0 copy-done.1
  (5 shorter events, 0.0 us)
Async XLA Ops:
  6.5 10.5 copy-start
  6.5 63.2 %all-gather.4.cloned.1.call-start = ((), (), s32[]{:S(2)}) async-start(), calls=%async_computation | async-start | bytes 3096576 | tf_op jit(solution)/shard_map/all_gather | solution.py:40
  13.3 0.8 copy-start.2
  13.3 1749.7 %all-gather.6.cloned.1.call-start = ((), (), s32[]{:S(2)}) async-start(), calls=%async_computation.2 | async-start | bytes 128450560 | tf_op jit(solution)/shard_map/all_gather | solution.py:13
  14.0 2862.1 %all-reduce.6.cloned.1.call-start = ((), (), s32[]{:S(2)}) async-start(), calls=%async_computation.1 | async-start | bytes 58720256 | tf_op jit(solution)/shard_map/psum | solution.py:57
  2876.1 23.3 copy-start.1
Sparse Core Ops, SparseCore 0:
  13.4 52.2 all-gather.3
  67.3 1695.6 all-gather.5
  1909.9 966.1 all-reduce.5
